TPU v7x, 32 devices: a whole 2x2x4 slice. The times are simulated.
32 devices in a mesh: grp: 2 (over y), seq: 16 (over z, x, core).
Axes of the slice: x: 2, y: 2, z: 4, core: 2. Of those that a mesh axis runs over, the one named last changes fastest.
Arguments:
- frames: bfloat16 [4, 10240, 1280], P('grp', 'seq'), parts along dimension 0, may hold values from -120 to 120
- dec_states: bfloat16 [2, 256, 1280], P(None, 'grp'), parts along dimension 1, may hold values from -6 to 6
- w_query: bfloat16 [1280, 1280], P(None, 'seq'), may hold values from -0.15625 to 0.15625
- w_keyval: bfloat16 [1280, 2560], replicated, may hold values from -0.15625 to 0.15625
- w_output: bfloat16 [1280, 1280], P(None, 'seq'), may hold values from -0.15625 to 0.15625
- head_slope: float32 [20], replicated, may hold values from 0.3 to 12
- lengths: int32 [4, 16], P('grp'), parts along dimension 0, may hold values from 128 to 640, as said below
- positions: int32 [2, 256], P(None, 'grp'), parts along dimension 1, may hold values from 0 to 15
Outputs:
- attended: bfloat16 [2, 256, 1280], P(None, 'grp', 'seq'), parts along dimension 1
There are 2 independent parts, one for each index of `grp`. A program takes and returns all parts, laid end to end along the dimension named above; an argument that names none is the same for every part. Nothing has to cross between parts.
Inputs may be any that keep to these rules, and one draw needn't show every extreme that they name: `lengths`: every step has one block of exactly 640 valid frames.
All inputs are finite; a program needn't handle non-finite values.
Results may differ from a plain program's by a relative error of at most 0.005.
The roundings to bfloat16 on the way count: a program that leaves them out, or rounds other values in their place, can miss the bound.
Values may be sent and summed in bfloat16 or wider, within the bound.
A program may use at most 128 MiB of HBM per device.

v0:
```python
import functools
import math
import jax
import jax.numpy as jnp
from jax import lax
from jax.sharding import PartitionSpec as P


def block_partial(
    queries,
    block_keys,
    block_values,
    length_now,
    slot_place,
    age_steps,
    row_positions,
    head_slope,
    devices,
):
    query_rows, head_count, head_size = queries.shape
    frame_count = block_keys.shape[0]
    keys_split = block_keys.reshape(frame_count, head_count, head_size)
    scores = jnp.einsum(
        "qhd,jhd->hqj", queries, keys_split, preferred_element_type=jnp.float32
    ) / math.sqrt(head_size)
    distance = (
        jnp.abs(row_positions.astype(jnp.float32) - slot_place.astype(jnp.float32)) / devices
        + age_steps
    )
    scores = scores - head_slope[:, None, None] * distance[None, :, None]
    valid = lax.broadcasted_iota(jnp.int32, (1, 1, frame_count), 2) < length_now
    scores = jnp.where(valid, scores, -jnp.inf)
    row_peak = jnp.max(scores, axis=2)
    weights = jnp.exp(scores - row_peak[:, :, None]).astype(jnp.bfloat16)
    row_total = jnp.sum(weights.astype(jnp.float32), axis=2)
    values_split = block_values.reshape(frame_count, head_count, head_size)
    row_context = jnp.einsum(
        "hqj,jhd->qhd", weights, values_split, preferred_element_type=jnp.float32
    )
    return (row_peak.T, row_total.T, row_context.reshape(query_rows, head_count * head_size))


def rescale(row_context, factors, head_count):
    query_rows = row_context.shape[0]
    spread_rows = row_context.reshape(query_rows, head_count, -1) * factors[:, :, None]
    return spread_rows.reshape(query_rows, -1)


def combine_parts(head_count, earlier, later):
    peak_one, total_one, context_one = earlier
    peak_two, total_two, context_two = later
    row_top = jnp.maximum(peak_one, peak_two)
    scale_one = jnp.exp(peak_one - row_top)
    scale_two = jnp.exp(peak_two - row_top)
    merged_total = total_one * scale_one + total_two * scale_two
    merged_context = rescale(context_one, scale_one, head_count) + rescale(
        context_two, scale_two, head_count
    )
    return (row_top, merged_total, merged_context)


def local(frames, dec_states, w_query, w_keyval, w_output, head_slope, lengths, positions):
    devices = lax.axis_size("seq")
    own_index = lax.axis_index("seq")
    step_count, frame_count, model_width = frames.shape
    query_rows = dec_states.shape[1]
    head_count = head_slope.shape[0]
    head_size = model_width // head_count
    frame_rows = frames.reshape(step_count * frame_count, model_width)
    keyval = jnp.dot(frame_rows, w_keyval, preferred_element_type=jnp.float32).astype(jnp.bfloat16)
    block_keys = keyval[:, :model_width].reshape(step_count, frame_count, model_width)
    block_values = keyval[:, model_width:].reshape(step_count, frame_count, model_width)
    dec_rows = dec_states.reshape(step_count * query_rows, model_width)
    local_query = jnp.dot(dec_rows, w_query, preferred_element_type=jnp.float32).astype(
        jnp.bfloat16
    )
    queries = lax.all_gather(local_query, "seq", axis=1, tiled=True)
    queries = queries.reshape(step_count, query_rows, head_count, head_size)
    combine = functools.partial(combine_parts, head_count)
    slot_place = (own_index + 1) % devices
    results = []
    for step_now in range(step_count):
        running = None
        for older_step in range(step_now + 1):
            partial_now = block_partial(
                queries[step_now],
                block_keys[older_step],
                block_values[older_step],
                lengths[older_step, own_index],
                slot_place,
                float(step_now - older_step),
                positions[step_now],
                head_slope,
                devices,
            )
            running = partial_now if running is None else combine(running, partial_now)
        row_peak, row_total, row_context = running
        row_top = lax.pmax(row_peak, "seq")
        factors = jnp.exp(row_peak - row_top)
        row_total, row_context = lax.psum(
            (row_total * factors, rescale(row_context, factors, head_count)), "seq"
        )
        context = row_context.reshape(query_rows, head_count, head_size) / row_total[:, :, None]
        context = context.reshape(query_rows, model_width).astype(jnp.bfloat16)
        results.append(
            jnp.dot(context, w_output, preferred_element_type=jnp.float32).astype(jnp.bfloat16)
        )
    return jnp.stack(results)


def solution(mesh):
    return jax.shard_map(
        local,
        mesh=mesh,
        in_specs=(
            P("grp", "seq", None),
            P(None, "grp", None),
            P(None, "seq"),
            P(),
            P(None, "seq"),
            P(),
            P("grp", None),
            P(None, "grp"),
        ),
        out_specs=P(None, "grp", "seq"),
        check_vma=False,
    )
```

profile of v0, /device:TPU:0, one launch (start us, length us, event | category | flops | bytes accessed | tf_op | source)
XLA Modules:
  0.0 259.9 jit_solution(2014881977530584230)
XLA Ops:
  6.5 0.8 broadcast_add_fusion
  7.4 0.8 multiply_bitcast_fusion.1
  8.2 1.4 constant_dynamic-slice_fusion.1
  9.6 0.6 iota_compare_fusion.1
  10.3 10.8 %convolution_convert_fusion = bf16[1280,2560]{1,0:T(8,128)(2,1)S(1)} fusion(bf16[1280,1280]{1,0:T(8,128)(2,1)S(1)} %bitcast.89, bf16[1280,2560]{1,0:T(8,128)(2,1)} %param.11), kind=kOutput, calls=%fused_computation | convolution fusion | flops 8391884800 | bytes 16384000 | tf_op jit(solution)/shard_map/dot_general | solution.py:70
  21.1 2.8 %fusion.18 = (bf16[640,1280]{1,0:T(8,128)(2,1)}, bf16[640,1280]{1,0:T(8,128)(2,1)}, bf16[640,1280]{1,0:T(8,128)(2,1)}, bf16[640,1280]{1,0:T(8,128)(2,1)}) fusion(bf16[1280,2560]{1,0:T(8,128)(2,1)S(1)} %convolution_convert_fusion), kind=kLoop, calls=%fused_computation.53 | loop fusion | bytes 13107200 | tf_op jit(solution)/shard_map/slice | solution.py:88
  23.9 3.5 %copy.16 = bf16[640,1280]{0,1:T(8,128)(2,1)} copy(bf16[640,1280]{1,0:T(8,128)(2,1)} %get-tuple-element.26) | data formatting | bytes 3276800 | tf_op jit(solution)/shard_map/slice | solution.py:87
  27.4 1.4 convolution_convert_fusion.1
  28.9 25.1 %all_gather.3 = bf16[256,1280]{0,1:T(8,128)(2,1)S(1)} all-gather(bf16[256,80]{0,1:T(8,128)(2,1)S(1)} %convolution_convert_fusion.1), channel_id=1, replica_groups=mesh['grp'=2,'seq'=16] {'seq'}, dimensions={1}, use_global_device_ids=true | all-gather | bytes 696320 | tf_op jit(solution)/shard_map/all_gather | solution.py:77
  54.0 0.9 fusion.19
  54.9 0.6 iota_compare_fusion
  55.5 3.5 %copy.17 = bf16[640,1280]{0,1:T(8,128)(2,1)} copy(bf16[640,1280]{1,0:T(8,128)(2,1)} %get-tuple-element.25) | data formatting | bytes 3276800 | tf_op jit(solution)/shard_map/slice | solution.py:87
  59.1 2.7 %fusion.20 = f32[20,128,640]{2,1,0:T(8,128)S(1)} fusion(bf16[128,20,64]{0,2,1:T(8,128)(2,1)} %bitcast.98, bf16[640,20,64]{0,2,1:T(8,128)(2,1)} %bitcast.92), kind=kOutput, calls=%fused_computation.55 | convolution fusion | flops 209715200 | bytes 8519680 | tf_op jit(solution)/shard_map/qhd,jhd->hqj/dot_general | solution.py:23
  61.9 1.6 fusion.2
  63.5 1.0 copy-done.3
  64.5 0.3 copy-done.9
  64.8 4.6 %fusion = (f32[20,128]{1,0:T(8,128)S(1)}, f32[20,128]{1,0:T(8,128)S(1)}, f32[20,128,640]{2,1,0:T(8,128)}) fusion(f32[20,128]{1,0:T(8,128)S(1)} %get-tuple-element.33, pred[640]{0:T(1024)(128)(4,1)S(1)} %iota_compare_fusion.1, f32[20,128]{1,0:T(8,128)S(1)} %get-tuple-element.31, f32[20,128,640]{2,1,0:T(8,128)S(1)} %fusion.20, ...), kind=kOutput, calls=%fused_computation.10 | convolution fusion | flops 222817280 | bytes 15114880 | tf_op jit(solution)/shard_map/qhd,jhd->hqj/dot_general | solution.py:23
  69.4 2.0 convert_reduce_fusion
  71.4 3.5 %copy.15 = bf16[640,1280]{0,1:T(8,128)(2,1)} copy(bf16[640,1280]{1,0:T(8,128)(2,1)} %get-tuple-element.23) | data formatting | bytes 3276800 | tf_op jit(solution)/shard_map/slice | solution.py:88
  74.9 3.5 %copy.18 = bf16[640,1280]{0,1:T(8,128)(2,1)} copy(bf16[640,1280]{1,0:T(8,128)(2,1)} %get-tuple-element.24) | data formatting | bytes 3276800 | tf_op jit(solution)/shard_map/slice | solution.py:88
  78.4 7.1 %convert_reduce_fusion.2 = (f32[20,128]{1,0:T(8,128)S(1)}, f32[20,128]{1,0:T(8,128)S(1)}) fusion(f32[20,128]{1,0:T(8,128)S(1)} %get-tuple-element.7, f32[20,128]{1,0:T(8,128)S(1)} %get-tuple-element.33, f32[20,128,640]{2,1,0:T(8,128)} %get-tuple-element.36, pred[640]{0:T(1024)(128)(4,1)S(1)} %iota_compare_fusion.1, f32[20,128]{1,0:T(8,128)S(1)} %get-tuple-element.8, ...), kind=kLoop, calls=%fused_computation.7 | loop fusion | flops 22932480 | bytes 13169280 | tf_op jit(solution)/shard_map/reduce_sum | solution.py:35
  85.5 57.8 %all-reduce.2 = (f32[128,20]{0,1:T(8,128)S(1)}, f32[128,20]{0,1:T(8,128)S(1)}) all-reduce(f32[128,20]{0,1:T(8,128)S(1)} %bitcast_maximum_fusion, f32[128,20]{0,1:T(8,128)S(1)} %bitcast.104), channel_id=1, replica_groups=mesh['grp'=2,'seq'=16] {'seq'}, use_global_device_ids=true, to_apply=%region_7.8 | all-reduce | flops 5120 | bytes 40960 | tf_op jit(solution)/shard_map/pmax | solution.py:98
  143.4 6.2 %fusion.3 = f32[128,20,64]{0,2,1:T(8,128)} fusion(bf16[640,20,64]{0,2,1:T(8,128)(2,1)} %bitcast.94, f32[128,20]{0,1:T(8,128)S(1)} %get-tuple-element.38, f32[20,128,640]{2,1,0:T(8,128)} %get-tuple-element.36, f32[20,128]{1,0:T(8,128)S(1)} %get-tuple-element.7, f32[20,128]{1,0:T(8,128)S(1)} %get-tuple-element.33, pred[640]{0:T(1024)(128)(4,1)S(1)} %iota_compare_fusion.1), kind=kOutput, calls=%fused_computation.16 | convolution fusion | flops 218071040 | bytes 8878720 | tf_op jit(solution)/shard_map/hqj,jhd->qhd/dot_general | solution.py:37
  149.6 4.3 %fusion.7 = f32[128,20,64]{0,2,1:T(8,128)S(1)} fusion(bf16[640,20,64]{0,2,1:T(8,128)(2,1)S(1)} %bitcast.96, f32[128,20]{0,1:T(8,128)S(1)} %get-tuple-element.20, f32[20,128,640]{2,1,0:T(8,128)} %copy-done.2, f32[20,128]{1,0:T(8,128)S(1)} %get-tuple-element.34, f32[20,128]{1,0:T(8,128)S(1)} %get-tuple-element.32, pred[640]{0:T(1024)(128)(4,1)S(1)} %iota_compare_fusion), kind=kOutput, calls=%fused_computation.20 | convolution fusion | flops 218071040 | bytes 8878720 | tf_op jit(solution)/shard_map/hqj,jhd->qhd/dot_general | solution.py:37
  153.9 0.3 copy-done.4
  154.2 0.7 slice-done.1
  154.9 2.9 %fusion.6 = f32[128,20,64]{0,2,1:T(8,128)} fusion(f32[128,20,64]{0,2,1:T(8,128)S(1)} %fusion.7, bf16[640,20,64]{0,2,1:T(8,128)(2,1)S(1)} %bitcast.95, f32[128,20]{0,1:T(8,128)S(1)} %get-tuple-element.19, f32[128,20]{0,1:T(8,128)S(1)} %get-tuple-element.18, f32[20,128,640]{2,1,0:T(8,128)S(1)} %bitcast.91, f32[20,128]{1,0:T(8,128)S(1)} %get-tuple-element.8, ...), kind=kOutput, calls=%fused_computation.19 | convolution fusion | flops 218398720 | bytes 9544320 | tf_op jit(solution)/shard_map/hqj,jhd->qhd/dot_general | solution.py:37
  157.9 58.0 %all-reduce = (f32[128,20]{0,1:T(8,128)S(1)}, f32[128,20]{0,1:T(8,128)S(1)}) all-reduce(f32[128,20]{0,1:T(8,128)S(1)} %get-tuple-element.17, f32[128,20]{0,1:T(8,128)S(1)} %get-tuple-element.37), channel_id=1, replica_groups=mesh['grp'=2,'seq'=16] {'seq'}, use_global_device_ids=true, to_apply=%region_11.12 | all-reduce | flops 5120 | bytes 40960 | tf_op jit(solution)/shard_map/psum | solution.py:100
  215.9 33.8 %all-reduce.5.cloned.1.call-done = (f32[128,1280]{0,1:T(8,128)}, f32[128,1280]{0,1:T(8,128)}) async-done(((f32[128,1280]{0,1:T(8,128)}, f32[128,1280]{0,1:T(8,128)}), (f32[128,1280]{0,1:T(8,128)}, f32[128,1280]{0,1:T(8,128)})) %all-reduce.5.cloned.1.call-update) | async-done | bytes 1310736 | tf_op jit(solution)/shard_map/psum | solution.py:100
  249.7 1.1 fusion.11
  251.0 1.1 fusion.10
  252.4 0.6 pad_maximum_fusion
  (32 shorter events, 0.6 us)
Async XLA Ops:
  6.5 3.7 %copy-start = (bf16[2,640,1280]{2,1,0:T(8,128)(2,1)S(1)}, bf16[2,640,1280]{2,1,0:T(8,128)(2,1)}, u32[]{:S(2)}) copy-start(bf16[2,640,1280]{2,1,0:T(8,128)(2,1)} %param.8) | copy-start | bytes 9830404
  6.5 243.1 %all-reduce.5.cloned.1.call-start = ((), (), s32[]{:S(2)}) async-start(), calls=%async_computation | async-start | bytes 2621440 | tf_op jit(solution)/shard_map/psum | solution.py:100
  21.1 6.3 %copy-start.10 = (bf16[1280,80]{0,1:T(8,128)(2,1)S(1)}, bf16[1280,80]{0,1:T(8,128)(2,1)}, u32[]{:S(2)}) copy-start(bf16[1280,80]{0,1:T(8,128)(2,1)} %param.10) | copy-start | bytes 614404
  54.0 7.9 %copy-start.11 = (f32[20]{0:T(128)S(1)}, f32[20]{0:T(128)}, u32[]{:S(2)}) copy-start(f32[20]{0:T(128)} %param.13) | copy-start | bytes 244
  59.1 2.9 %copy-start.6 = (bf16[640,1280]{0,1:T(8,128)(2,1)S(1)}, bf16[640,1280]{0,1:T(8,128)(2,1)}, u32[]{:S(2)}) copy-start(bf16[640,1280]{0,1:T(8,128)(2,1)} %copy.17) | copy-start | bytes 4915204
  59.1 2.9 %copy-start.7 = (bf16[128,1280]{0,1:T(8,128)(2,1)S(1)}, bf16[128,1280]{0,1:T(8,128)(2,1)}, u32[]{:S(2)}) copy-start(bf16[128,1280]{0,1:T(8,128)(2,1)} %get-tuple-element.28) | copy-start | bytes 983044
  61.8 7.5 %copy-start.1 = (f32[20,128,640]{2,1,0:T(8,128)}, f32[20,128,640]{2,1,0:T(8,128)S(1)}, u32[]{:S(2)}) copy-start(f32[20,128,640]{2,1,0:T(8,128)S(1)} %fusion.20) | copy-start | bytes 19660804
  61.8 2.6 %copy-start.3 = (bf16[640,1280]{0,1:T(8,128)(2,1)S(1)}, bf16[640,1280]{0,1:T(8,128)(2,1)}, u32[]{:S(2)}) copy-start(bf16[640,1280]{0,1:T(8,128)(2,1)} %copy.16) | copy-start | bytes 4915204
  61.8 2.9 %copy-start.9 = (bf16[128,1280]{0,1:T(8,128)(2,1)S(1)}, bf16[128,1280]{0,1:T(8,128)(2,1)}, u32[]{:S(2)}) copy-start(bf16[128,1280]{0,1:T(8,128)(2,1)} %get-tuple-element.27) | copy-start | bytes 983044
  63.5 5.9 %copy-start.2 = (f32[20,128,640]{2,1,0:T(8,128)}, f32[20,128,640]{2,1,0:T(8,128)S(1)}, u32[]{:S(2)}) copy-start(f32[20,128,640]{2,1,0:T(8,128)S(1)} %get-tuple-element.35) | copy-start | bytes 19660804
  143.3 6.3 %copy-start.5 = (bf16[640,1280]{0,1:T(8,128)(2,1)S(1)}, bf16[640,1280]{0,1:T(8,128)(2,1)}, u32[]{:S(2)}) copy-start(bf16[640,1280]{0,1:T(8,128)(2,1)} %copy.18) | copy-start | bytes 4915204
  149.6 4.3 %slice-start = ((s8[6553600]{0:T(1024)(128)(4,1)}), s8[4194304]{0:T(1024)(128)(4,1)S(1)}, s32[]{:S(2)}) async-start(s8[6553600]{0:T(1024)(128)(4,1)} %bitcast.90), calls=%async_computation.1 | async-start | bytes 8388608
  149.6 4.6 %copy-start.4 = (bf16[640,1280]{0,1:T(8,128)(2,1)S(1)}, bf16[640,1280]{0,1:T(8,128)(2,1)}, u32[]{:S(2)}) copy-start(bf16[640,1280]{0,1:T(8,128)(2,1)} %copy.15) | copy-start | bytes 4915204
  149.6 5.3 %slice-start.1 = ((s8[6553600]{0:T(1024)(128)(4,1)}), s8[2359296]{0:T(1024)(128)(4,1)S(1)}, s32[]{:S(2)}) async-start(s8[6553600]{0:T(1024)(128)(4,1)} %bitcast.90), calls=%async_computation.2 | async-start | bytes 4718592
  154.9 95.9 %copy-start.8 = (bf16[1280,80]{0,1:T(8,128)(2,1)S(1)}, bf16[1280,80]{0,1:T(8,128)(2,1)}, u32[]{:S(2)}) copy-start(bf16[1280,80]{0,1:T(8,128)(2,1)} %param.12) | copy-start | bytes 614404
Sparse Core Ops, SparseCore 0:
  158.0 91.5 all-reduce.4
where the time goes:
time: 260 us
  blocking collectives  141 us (54%)
  matrix products  35 us (13%)
  waiting for transfers between devices  33.8 us (13%)
  local copies, waits for them, and re-layouts  21.6 us (8%)
  other arithmetic  15.1 us (6%)
  between operations  13.6 us (5%)
    psum x1, blocking collectives, local(): lax.psum((row_total * factors, rescale(row_context, factors, head_count))...  58 us
    pmax x1, blocking collectives, local(): row_top = lax.pmax(row_peak, 'seq')  57.8 us
    psum x1, waiting for transfers between devices, local(): lax.psum((row_total * factors, rescale(row_context, factors, head_count))...  33.8 us
    all_gather x1, blocking collectives, local(): queries = lax.all_gather(local_query, 'seq', axis=1, tiled=True)  25.1 us
    dot_general x3, matrix products, block_partial(): jnp.einsum('hqj,jhd->qhd', weights, values_split, preferred_element_type=...  13.5 us
    dot_general x1, matrix products, local(): jnp.dot(frame_rows, w_keyval, preferred_element_type=jnp.float32)  10.8 us
    slice x3, local copies, waits for them, and re-layouts, local(): block_values[older_step]  9.87 us
    reduce_sum x2, other arithmetic, block_partial(): row_total = jnp.sum(weights.astype(jnp.float32), axis=2)  9.08 us
  transfers between devices with their start and end apart: 1, of which 1 were waited for; matrix products, arithmetic and copies ran while one was open for 0% of the time, Pallas kernels for 0%

commit v1 on v0

--- a/solution.py
+++ b/solution.py
@@ -74,7 +74,8 @@
     local_query = jnp.dot(dec_rows, w_query, preferred_element_type=jnp.float32).astype(
         jnp.bfloat16
     )
-    queries = lax.all_gather(local_query, "seq", axis=1, tiled=True)
+    form_block = lambda m: jnp.concatenate(jax.lax.all_gather(m, "seq"), 1)
+    queries = form_block(local_query)
     queries = queries.reshape(step_count, query_rows, head_count, head_size)
     combine = functools.partial(combine_parts, head_count)
     slot_place = (own_index + 1) % devices

time: 260 us -> 262 us (level)
  no operation moved by 1% of the time
where the time goes in v1:
time: 262 us; the launch traced here: 261 us
  blocking collectives  141 us (54%)
  matrix products  35 us (13%)
  waiting for transfers between devices  33.8 us (13%)
  local copies, waits for them, and re-layouts  22.5 us (9%)
  other arithmetic  15.1 us (6%)
  between operations  13.6 us (5%)
    psum x1, blocking collectives, local(): lax.psum((row_total * factors, rescale(row_context, factors, head_count))...  58 us
    pmax x1, blocking collectives, local(): row_top = lax.pmax(row_peak, 'seq')  57.8 us
    psum x1, waiting for transfers between devices, local(): lax.psum((row_total * factors, rescale(row_context, factors, head_count))...  33.8 us
    all_gather x1, blocking collectives, local(): form_block = lambda m: jnp.concatenate(jax.lax.all_gather(m, 'seq'), 1)  25.3 us
    dot_general x3, matrix products, block_partial(): jnp.einsum('hqj,jhd->qhd', weights, values_split, preferred_element_type=...  13.5 us
    dot_general x1, matrix products, local(): jnp.dot(frame_rows, w_keyval, preferred_element_type=jnp.float32)  10.8 us
    slice x3, local copies, waits for them, and re-layouts, local(): block_values[older_step]  9.87 us
    reduce_sum x2, other arithmetic, block_partial(): row_total = jnp.sum(weights.astype(jnp.float32), axis=2)  9.08 us
  transfers between devices with their start and end apart: 1, of which 1 were waited for; matrix products, arithmetic and copies ran while one was open for 0% of the time, Pallas kernels for 0%

profile of v1, /device:TPU:0, one launch (start us, length us, event | category | flops | bytes accessed | tf_op | source)
XLA Modules:
  0.0 261.0 jit_solution(10012711353919975479)
XLA Ops:
  6.5 0.8 broadcast_add_fusion
  7.4 0.8 multiply_bitcast_fusion.1
  8.2 1.4 constant_dynamic-slice_fusion.1
  9.6 0.6 iota_compare_fusion.1
  10.3 10.8 %convolution_convert_fusion = bf16[1280,2560]{1,0:T(8,128)(2,1)S(1)} fusion(bf16[1280,1280]{1,0:T(8,128)(2,1)S(1)} %bitcast.95, bf16[1280,2560]{1,0:T(8,128)(2,1)} %param.11), kind=kOutput, calls=%fused_computation | convolution fusion | flops 8391884800 | bytes 16384000 | tf_op jit(solution)/shard_map/dot_general | solution.py:70
  21.1 2.8 %fusion.18 = (bf16[640,1280]{1,0:T(8,128)(2,1)}, bf16[640,1280]{1,0:T(8,128)(2,1)}, bf16[640,1280]{1,0:T(8,128)(2,1)}, bf16[640,1280]{1,0:T(8,128)(2,1)}) fusion(bf16[1280,2560]{1,0:T(8,128)(2,1)S(1)} %convolution_convert_fusion), kind=kLoop, calls=%fused_computation.53 | loop fusion | bytes 13107200 | tf_op jit(solution)/shard_map/slice | solution.py:89
  23.9 3.5 %copy.19 = bf16[640,1280]{0,1:T(8,128)(2,1)} copy(bf16[640,1280]{1,0:T(8,128)(2,1)} %get-tuple-element.26) | data formatting | bytes 3276800 | tf_op jit(solution)/shard_map/slice | solution.py:88
  27.4 1.4 convolution_convert_fusion.1
  28.9 25.3 %all-gather = bf16[4096,80]{0,1:T(8,128)(2,1)S(1)} all-gather(bf16[256,80]{0,1:T(8,128)(2,1)S(1)} %convolution_convert_fusion.1), channel_id=2, replica_groups=mesh['grp'=2,'seq'=16] {'seq'}, dimensions={0}, use_global_device_ids=true | all-gather | bytes 696320 | tf_op jit(solution)/shard_map/all_gather | solution.py:77
  54.4 0.8 copy.20
  55.2 0.8 copy.18
  56.0 0.6 iota_compare_fusion
  56.7 3.5 %copy.21 = bf16[640,1280]{0,1:T(8,128)(2,1)} copy(bf16[640,1280]{1,0:T(8,128)(2,1)} %get-tuple-element.25) | data formatting | bytes 3276800 | tf_op jit(solution)/shard_map/slice | solution.py:88
  60.2 2.7 %fusion.20 = f32[20,128,640]{2,1,0:T(8,128)S(1)} fusion(bf16[128,20,64]{0,2,1:T(8,128)(2,1)} %bitcast.106, bf16[640,20,64]{0,2,1:T(8,128)(2,1)} %bitcast.98), kind=kOutput, calls=%fused_computation.55 | convolution fusion | flops 209715200 | bytes 8519680 | tf_op jit(solution)/shard_map/qhd,jhd->hqj/dot_general | solution.py:23
  63.1 1.6 fusion.2
  64.7 1.0 copy-done.3
  65.9 4.6 %fusion = (f32[20,128]{1,0:T(8,128)S(1)}, f32[20,128]{1,0:T(8,128)S(1)}, f32[20,128,640]{2,1,0:T(8,128)}) fusion(f32[20,128]{1,0:T(8,128)S(1)} %get-tuple-element.33, pred[640]{0:T(1024)(128)(4,1)S(1)} %iota_compare_fusion.1, f32[20,128]{1,0:T(8,128)S(1)} %get-tuple-element.31, f32[20,128,640]{2,1,0:T(8,128)S(1)} %fusion.20, ...), kind=kOutput, calls=%fused_computation.10 | convolution fusion | flops 222817280 | bytes 15114880 | tf_op jit(solution)/shard_map/qhd,jhd->hqj/dot_general | solution.py:23
  70.5 2.0 convert_reduce_fusion
  72.6 3.5 %copy.17 = bf16[640,1280]{0,1:T(8,128)(2,1)} copy(bf16[640,1280]{1,0:T(8,128)(2,1)} %get-tuple-element.23) | data formatting | bytes 3276800 | tf_op jit(solution)/shard_map/slice | solution.py:89
  76.1 3.5 %copy.22 = bf16[640,1280]{0,1:T(8,128)(2,1)} copy(bf16[640,1280]{1,0:T(8,128)(2,1)} %get-tuple-element.24) | data formatting | bytes 3276800 | tf_op jit(solution)/shard_map/slice | solution.py:89
  79.6 7.1 %convert_reduce_fusion.2 = (f32[20,128]{1,0:T(8,128)S(1)}, f32[20,128]{1,0:T(8,128)S(1)}) fusion(f32[20,128]{1,0:T(8,128)S(1)} %get-tuple-element.7, f32[20,128]{1,0:T(8,128)S(1)} %get-tuple-element.33, f32[20,128,640]{2,1,0:T(8,128)} %get-tuple-element.36, pred[640]{0:T(1024)(128)(4,1)S(1)} %iota_compare_fusion.1, f32[20,128]{1,0:T(8,128)S(1)} %get-tuple-element.8, ...), kind=kLoop, calls=%fused_computation.7 | loop fusion | flops 22932480 | bytes 13169280 | tf_op jit(solution)/shard_map/reduce_sum | solution.py:35
  86.7 57.8 %all-reduce.2 = (f32[128,20]{0,1:T(8,128)S(1)}, f32[128,20]{0,1:T(8,128)S(1)}) all-reduce(f32[128,20]{0,1:T(8,128)S(1)} %bitcast_maximum_fusion, f32[128,20]{0,1:T(8,128)S(1)} %bitcast.112), channel_id=1, replica_groups=mesh['grp'=2,'seq'=16] {'seq'}, use_global_device_ids=true, to_apply=%region_7.8 | all-reduce | flops 5120 | bytes 40960 | tf_op jit(solution)/shard_map/pmax | solution.py:99
  144.5 6.2 %fusion.3 = f32[128,20,64]{0,2,1:T(8,128)} fusion(bf16[640,20,64]{0,2,1:T(8,128)(2,1)} %bitcast.102, f32[128,20]{0,1:T(8,128)S(1)} %get-tuple-element.38, f32[20,128,640]{2,1,0:T(8,128)} %get-tuple-element.36, f32[20,128]{1,0:T(8,128)S(1)} %get-tuple-element.7, f32[20,128]{1,0:T(8,128)S(1)} %get-tuple-element.33, pred[640]{0:T(1024)(128)(4,1)S(1)} %iota_compare_fusion.1), kind=kOutput, calls=%fused_computation.16 | convolution fusion | flops 218071040 | bytes 8878720 | tf_op jit(solution)/shard_map/hqj,jhd->qhd/dot_general | solution.py:37
  150.8 4.3 %fusion.7 = f32[128,20,64]{0,2,1:T(8,128)S(1)} fusion(bf16[640,20,64]{0,2,1:T(8,128)(2,1)S(1)} %bitcast.104, f32[128,20]{0,1:T(8,128)S(1)} %get-tuple-element.20, f32[20,128,640]{2,1,0:T(8,128)} %copy-done.2, f32[20,128]{1,0:T(8,128)S(1)} %get-tuple-element.34, f32[20,128]{1,0:T(8,128)S(1)} %get-tuple-element.32, pred[640]{0:T(1024)(128)(4,1)S(1)} %iota_compare_fusion), kind=kOutput, calls=%fused_computation.20 | convolution fusion | flops 218071040 | bytes 8878720 | tf_op jit(solution)/shard_map/hqj,jhd->qhd/dot_general | solution.py:37
  155.1 0.3 copy-done.4
  155.4 0.7 slice-done.1
  156.1 2.9 %fusion.6 = f32[128,20,64]{0,2,1:T(8,128)} fusion(f32[128,20,64]{0,2,1:T(8,128)S(1)} %fusion.7, bf16[640,20,64]{0,2,1:T(8,128)(2,1)S(1)} %bitcast.103, f32[128,20]{0,1:T(8,128)S(1)} %get-tuple-element.19, f32[128,20]{0,1:T(8,128)S(1)} %get-tuple-element.18, f32[20,128,640]{2,1,0:T(8,128)S(1)} %bitcast.97, f32[20,128]{1,0:T(8,128)S(1)} %get-tuple-element.8, ...), kind=kOutput, calls=%fused_computation.19 | convolution fusion | flops 218398720 | bytes 9544320 | tf_op jit(solution)/shard_map/hqj,jhd->qhd/dot_general | solution.py:37
  159.1 58.0 %all-reduce = (f32[128,20]{0,1:T(8,128)S(1)}, f32[128,20]{0,1:T(8,128)S(1)}) all-reduce(f32[128,20]{0,1:T(8,128)S(1)} %get-tuple-element.17, f32[128,20]{0,1:T(8,128)S(1)} %get-tuple-element.37), channel_id=1, replica_groups=mesh['grp'=2,'seq'=16] {'seq'}, use_global_device_ids=true, to_apply=%region_11.12 | all-reduce | flops 5120 | bytes 40960 | tf_op jit(solution)/shard_map/psum | solution.py:101
  217.1 33.8 %all-reduce.5.cloned.1.call-done = (f32[128,1280]{0,1:T(8,128)}, f32[128,1280]{0,1:T(8,128)}) async-done(((f32[128,1280]{0,1:T(8,128)}, f32[128,1280]{0,1:T(8,128)}), (f32[128,1280]{0,1:T(8,128)}, f32[128,1280]{0,1:T(8,128)})) %all-reduce.5.cloned.1.call-update) | async-done | bytes 1310736 | tf_op jit(solution)/shard_map/psum | solution.py:101
  250.8 1.1 fusion.11
  252.2 1.1 fusion.10
  253.6 0.6 pad_maximum_fusion
  (35 shorter events, 1.1 us)
Async XLA Ops:
  6.5 3.7 %copy-start = (bf16[2,640,1280]{2,1,0:T(8,128)(2,1)S(1)}, bf16[2,640,1280]{2,1,0:T(8,128)(2,1)}, u32[]{:S(2)}) copy-start(bf16[2,640,1280]{2,1,0:T(8,128)(2,1)} %param.8) | copy-start | bytes 9830404
  6.5 244.3 %all-reduce.5.cloned.1.call-start = ((), (), s32[]{:S(2)}) async-start(), calls=%async_computation | async-start | bytes 2621440 | tf_op jit(solution)/shard_map/psum | solution.py:101
  21.1 6.3 %copy-start.10 = (bf16[1280,80]{0,1:T(8,128)(2,1)S(1)}, bf16[1280,80]{0,1:T(8,128)(2,1)}, u32[]{:S(2)}) copy-start(bf16[1280,80]{0,1:T(8,128)(2,1)} %param.10) | copy-start | bytes 614404
  54.4 8.6 %copy-start.11 = (f32[20]{0:T(128)S(1)}, f32[20]{0:T(128)}, u32[]{:S(2)}) copy-start(f32[20]{0:T(128)} %param.13) | copy-start | bytes 244
  60.2 2.9 %copy-start.6 = (bf16[640,1280]{0,1:T(8,128)(2,1)S(1)}, bf16[640,1280]{0,1:T(8,128)(2,1)}, u32[]{:S(2)}) copy-start(bf16[640,1280]{0,1:T(8,128)(2,1)} %copy.21) | copy-start | bytes 4915204
  60.2 2.9 %copy-start.7 = (bf16[128,16,80]{0,2,1:T(8,128)(2,1)S(1)}, bf16[128,16,80]{0,2,1:T(8,128)(2,1)}, u32[]{:S(2)}) copy-start(bf16[128,16,80]{0,2,1:T(8,128)(2,1)} %copy.20) | copy-start | bytes 983044
  63.0 7.5 %copy-start.1 = (f32[20,128,640]{2,1,0:T(8,128)}, f32[20,128,640]{2,1,0:T(8,128)S(1)}, u32[]{:S(2)}) copy-start(f32[20,128,640]{2,1,0:T(8,128)S(1)} %fusion.20) | copy-start | bytes 19660804
  63.0 2.6 %copy-start.3 = (bf16[640,1280]{0,1:T(8,128)(2,1)S(1)}, bf16[640,1280]{0,1:T(8,128)(2,1)}, u32[]{:S(2)}) copy-start(bf16[640,1280]{0,1:T(8,128)(2,1)} %copy.19) | copy-start | bytes 4915204
  63.0 2.9 %copy-start.9 = (bf16[128,16,80]{0,2,1:T(8,128)(2,1)S(1)}, bf16[128,16,80]{0,2,1:T(8,128)(2,1)}, u32[]{:S(2)}) copy-start(bf16[128,16,80]{0,2,1:T(8,128)(2,1)} %copy.18) | copy-start | bytes 983044
  64.7 5.9 %copy-start.2 = (f32[20,128,640]{2,1,0:T(8,128)}, f32[20,128,640]{2,1,0:T(8,128)S(1)}, u32[]{:S(2)}) copy-start(f32[20,128,640]{2,1,0:T(8,128)S(1)} %get-tuple-element.35) | copy-start | bytes 19660804
  144.5 6.3 %copy-start.5 = (bf16[640,1280]{0,1:T(8,128)(2,1)S(1)}, bf16[640,1280]{0,1:T(8,128)(2,1)}, u32[]{:S(2)}) copy-start(bf16[640,1280]{0,1:T(8,128)(2,1)} %copy.22) | copy-start | bytes 4915204
  150.8 4.3 %slice-start = ((s8[6553600]{0:T(1024)(128)(4,1)}), s8[4194304]{0:T(1024)(128)(4,1)S(1)}, s32[]{:S(2)}) async-start(s8[6553600]{0:T(1024)(128)(4,1)} %bitcast.96), calls=%async_computation.1 | async-start | bytes 8388608
  150.8 4.6 %copy-start.4 = (bf16[640,1280]{0,1:T(8,128)(2,1)S(1)}, bf16[640,1280]{0,1:T(8,128)(2,1)}, u32[]{:S(2)}) copy-start(bf16[640,1280]{0,1:T(8,128)(2,1)} %copy.17) | copy-start | bytes 4915204
  150.8 5.3 %slice-start.1 = ((s8[6553600]{0:T(1024)(128)(4,1)}), s8[2359296]{0:T(1024)(128)(4,1)S(1)}, s32[]{:S(2)}) async-start(s8[6553600]{0:T(1024)(128)(4,1)} %bitcast.96), calls=%async_computation.2 | async-start | bytes 4718592
  156.1 95.9 %copy-start.8 = (bf16[1280,80]{0,1:T(8,128)(2,1)S(1)}, bf16[1280,80]{0,1:T(8,128)(2,1)}, u32[]{:S(2)}) copy-start(bf16[1280,80]{0,1:T(8,128)(2,1)} %param.12) | copy-start | bytes 614404
Sparse Core Ops, SparseCore 0:
  159.2 91.5 all-reduce.4
